TPU v7x, 32 devices: a whole 2x2x4 slice. The times are simulated.
32 devices in a mesh: dp: 8 (over z, core), mp: 4 (over y, x).
Axes of the slice: x: 2, y: 2, z: 4, core: 2. Of those that a mesh axis runs over, the one named last changes fastest.
Arguments:
- features: bfloat16 [8192, 8192], P('dp', 'mp'), may hold values from -6 to 6
- v_weight: bfloat16 [3, 8192, 1024], P(None, 'mp', 'dp'), may hold values from -0.0625 to 0.0625
- u_weight: bfloat16 [3, 1024, 8192], P(None, 'dp', 'mp'), may hold values from -0.1875 to 0.1875
- cross_bias: float32 [3, 8192], P(None, 'mp'), may hold values from -3 to 3
Outputs:
- crossed: bfloat16 [8192, 8192], P('dp', 'mp')
All inputs are finite; a program needn't handle non-finite values.
Results may differ from a plain program's by a relative error of at most 0.009.
Values may be sent and summed in bfloat16 or wider, within the bound.
A program may use at most 128 MiB of HBM per device.

v0:
```python
import jax
import jax.numpy as jnp
from jax import lax
from jax.sharding import PartitionSpec as P


def local(features, v_weight, u_weight, cross_bias):
    carried = features
    layers = v_weight.shape[0]
    for layer_number in range(layers):
        current = carried
        partial_value = jnp.dot(
            current,
            lax.all_gather(v_weight[layer_number], "dp", axis=1, tiled=True),
            preferred_element_type=jnp.float32,
        )
        rank_proj = lax.psum(partial_value, "mp").astype(jnp.bfloat16)
        cross_term = jnp.dot(
            rank_proj,
            lax.all_gather(u_weight[layer_number], "dp", axis=0, tiled=True),
            preferred_element_type=jnp.float32,
        )
        cross_term = cross_term + cross_bias[layer_number]
        carried = (features.astype(jnp.float32) * cross_term + current.astype(jnp.float32)).astype(
            jnp.bfloat16
        )
    return carried


def solution(mesh):
    return jax.shard_map(
        local,
        mesh=mesh,
        in_specs=(P("dp", "mp"), P(None, "mp", "dp"), P(None, "dp", "mp"), P(None, "mp")),
        out_specs=P("dp", "mp"),
        check_vma=False,
    )
```

profile of v0, /device:TPU:0, one launch (start us, length us, event | category | flops | bytes accessed | tf_op | source)
XLA Modules:
  0.0 553.8 jit_solution(13807894456703240402)
XLA Ops:
  6.5 0.0 copy-start
  6.5 0.0 copy-start.1
  6.5 0.0 all-gather.13.cloned.1.call-start
  6.5 2.6 fusion.26
  9.2 0.0 all-gather.13.cloned.1.call-update
  9.2 0.0 all-gather.15.cloned.1.call-start
  9.3 0.0 copy-done
  9.3 1.2 fusion.27
  10.5 0.0 all-gather.15.cloned.1.call-update
  10.5 0.0 all-gather.17.cloned.1.call-start
  10.6 0.7 all-gather.17.cloned.1.call-update
  11.2 0.0 all-gather.19.cloned.1.call-start
  11.3 0.5 all-gather.19.cloned.1.call-update
  11.8 0.0 all-gather.21.cloned.1.call-start
  11.9 0.5 all-gather.21.cloned.1.call-update
  12.4 0.0 all-gather.23.cloned.1.call-start
  12.5 0.5 all-gather.23.cloned.1.call-update
  13.0 0.0 copy-done.1
  13.0 46.9 %all-gather.13.cloned.1.call-done = bf16[1,2048,1024]{2,1,0:T(8,128)(2,1)} async-done(((bf16[1,2048,128]{2,1,0:T(8,128)(2,1)}), bf16[1,2048,1024]{2,1,0:T(8,128)(2,1)}) %all-gather.13.cloned.1.call-update) | async-done | bytes 4194320 | tf_op jit(solution)/shard_map/all_gather | solution.py:14
  59.9 10.0 %fusion.15 = f32[1024,1024]{1,0:T(8,128)} fusion(bf16[1024,2048]{1,0:T(8,128)(2,1)} %param.4, bf16[1,2048,1024]{2,1,0:T(8,128)(2,1)} %all-gather.13.cloned.1.call-done), kind=kOutput, calls=%fused_computation.19 | convolution fusion | flops 4294967296 | bytes 12582912 | tf_op jit(solution)/shard_map/dot_general | solution.py:12
  69.9 145.6 %all-reduce.3 = bf16[1024,1024]{1,0:T(8,128)(2,1)S(1)} all-reduce(f32[1024,1024]{1,0:T(8,128)} %fusion.15), channel_id=1, replica_groups=mesh['dp'=8,'mp'=4] {'mp'}, use_global_device_ids=true, to_apply=%region_0.0 | all-reduce | flops 1048576 | bytes 6291456 | tf_op jit(solution)/shard_map/psum | solution.py:17
  215.5 0.0 all-gather.15.cloned.1.call-done
  215.6 9.2 %fusion = bf16[1024,2048]{1,0:T(8,128)(2,1)} fusion(bf16[1024,2048]{1,0:T(8,128)(2,1)} %param.4, f32[2048]{0:T(1024)S(1)} %bitcast.35, bf16[1,1024,2048]{2,1,0:T(8,128)(2,1)} %all-gather.15.cloned.1.call-done, bf16[1024,1024]{1,0:T(8,128)(2,1)S(1)} %all-reduce.3), kind=kOutput, calls=%fused_computation.4 | convolution fusion | flops 4305453056 | bytes 14688256 | tf_op jit(solution)/shard_map/dot_general | solution.py:18
  224.8 0.0 all-gather.17.cloned.1.call-done
  224.8 10.0 %fusion.11 = f32[1024,1024]{1,0:T(8,128)} fusion(bf16[1024,2048]{1,0:T(8,128)(2,1)} %fusion, bf16[1,2048,1024]{2,1,0:T(8,128)(2,1)} %all-gather.17.cloned.1.call-done), kind=kOutput, calls=%fused_computation.15 | convolution fusion | flops 4294967296 | bytes 12582912 | tf_op jit(solution)/shard_map/dot_general | solution.py:12
  234.8 142.2 %all-reduce.4 = bf16[1024,1024]{1,0:T(8,128)(2,1)S(1)} all-reduce(f32[1024,1024]{1,0:T(8,128)} %fusion.11), channel_id=1, replica_groups=mesh['dp'=8,'mp'=4] {'mp'}, use_global_device_ids=true, to_apply=%region_1.0 | all-reduce | flops 1048576 | bytes 6291456 | tf_op jit(solution)/shard_map/psum | solution.py:17
  377.1 0.0 all-gather.19.cloned.1.call-done
  377.1 9.9 %fusion.2 = bf16[1024,2048]{1,0:T(8,128)(2,1)} fusion(bf16[1024,2048]{1,0:T(8,128)(2,1)} %param.4, bf16[1024,2048]{1,0:T(8,128)(2,1)} %fusion, f32[2048]{0:T(1024)S(1)} %bitcast.34, bf16[1,1024,2048]{2,1,0:T(8,128)(2,1)} %all-gather.19.cloned.1.call-done, bf16[1024,1024]{1,0:T(8,128)(2,1)S(1)} %all-reduce.4), kind=kOutput, calls=%fused_computation.6 | convolution fusion | flops 4307550208 | bytes 18882560 | tf_op jit(solution)/shard_map/dot_general | solution.py:18
  387.0 0.0 all-gather.21.cloned.1.call-done
  387.0 9.9 %fusion.7 = f32[1024,1024]{1,0:T(8,128)} fusion(bf16[1024,2048]{1,0:T(8,128)(2,1)} %fusion.2, bf16[1,2048,1024]{2,1,0:T(8,128)(2,1)} %all-gather.21.cloned.1.call-done), kind=kOutput, calls=%fused_computation.11 | convolution fusion | flops 4294967296 | bytes 12582912 | tf_op jit(solution)/shard_map/dot_general | solution.py:12
  396.9 140.1 %all-reduce.5 = bf16[1024,1024]{1,0:T(8,128)(2,1)S(1)} all-reduce(f32[1024,1024]{1,0:T(8,128)} %fusion.7), channel_id=1, replica_groups=mesh['dp'=8,'mp'=4] {'mp'}, use_global_device_ids=true, to_apply=%region_2.0 | all-reduce | flops 1048576 | bytes 6291456 | tf_op jit(solution)/shard_map/psum | solution.py:17
  537.0 0.0 all-gather.23.cloned.1.call-done
  537.1 9.9 %fusion.4 = bf16[1024,2048]{1,0:T(8,128)(2,1)} fusion(bf16[1024,2048]{1,0:T(8,128)(2,1)} %param.4, bf16[1024,2048]{1,0:T(8,128)(2,1)} %fusion.2, f32[2048]{0:T(1024)S(1)} %bitcast.33, bf16[1,1024,2048]{2,1,0:T(8,128)(2,1)} %all-gather.23.cloned.1.call-done, bf16[1024,1024]{1,0:T(8,128)(2,1)S(1)} %all-reduce.5), kind=kOutput, calls=%fused_computation.8 | convolution fusion | flops 4307550208 | bytes 18882560 | tf_op jit(solution)/shard_map/dot_general | solution.py:18
  (1 shorter events, 0.0 us)
Async XLA Ops:
  6.5 2.7 copy-start
  6.5 6.4 %copy-start.1 = (f32[3,2048]{1,0:T(4,128)S(1)}, f32[3,2048]{1,0:T(4,128)}, u32[]{:S(2)}) copy-start(f32[3,2048]{1,0:T(4,128)} %param.7) | copy-start | bytes 73732
  6.5 53.4 %all-gather.13.cloned.1.call-start = ((), (), s32[]{:S(2)}) async-start(), calls=%async_computation | async-start | bytes 4718592 | tf_op jit(solution)/shard_map/all_gather | solution.py:14
  9.2 206.3 %all-gather.15.cloned.1.call-start = ((), (), s32[]{:S(2)}) async-start(), calls=%async_computation.1 | async-start | bytes 4718592 | tf_op jit(solution)/shard_map/all_gather | solution.py:20
  10.5 214.3 %all-gather.17.cloned.1.call-start = ((), (), s32[]{:S(2)}) async-start(), calls=%async_computation.2 | async-start | bytes 4718592 | tf_op jit(solution)/shard_map/all_gather | solution.py:14
  11.2 365.8 %all-gather.19.cloned.1.call-start = ((), (), s32[]{:S(2)}) async-start(), calls=%async_computation.3 | async-start | bytes 4718592 | tf_op jit(solution)/shard_map/all_gather | solution.py:20
  11.8 375.1 %all-gather.21.cloned.1.call-start = ((), (), s32[]{:S(2)}) async-start(), calls=%async_computation.4 | async-start | bytes 4718592 | tf_op jit(solution)/shard_map/all_gather | solution.py:14
  12.4 524.6 %all-gather.23.cloned.1.call-start = ((), (), s32[]{:S(2)}) async-start(), calls=%async_computation.5 | async-start | bytes 4718592 | tf_op jit(solution)/shard_map/all_gather | solution.py:20
Sparse Core Ops, SparseCore 0:
  9.3 50.5 all-gather.12
  61.5 45.0 all-gather.14
  108.2 46.6 all-gather.16
  156.3 45.0 all-gather.18
  202.8 46.6 all-gather.20
  250.9 45.0 all-gather.22
where the time goes:
time: 554 us
  blocking collectives  428 us (77%)
  matrix products  58.9 us (11%)
  waiting for transfers between devices  49.3 us (9%)
  between operations  13.5 us (2%)
    psum x3, blocking collectives, local(): rank_proj = lax.psum(partial_value, 'mp').astype(jnp.bfloat16)  428 us
    all_gather x3, waiting for transfers between devices, local(): lax.all_gather(v_weight[layer_number], 'dp', axis=1, tiled=True)  46.9 us
    dot_general x3, matrix products, local(): jnp.dot(current, lax.all_gather(v_weight[layer_number], 'dp', axis=1, til...  29.9 us
    dot_general x3, matrix products, local(): jnp.dot(rank_proj, lax.all_gather(u_weight[layer_number], 'dp', axis=0, t...  29 us
  transfers between devices with their start and end apart: 6, of which 1 were waited for; matrix products, arithmetic and copies ran while one was open for 9% of the time, Pallas kernels for 0%

commit v1 on v0

--- a/solution.py
+++ b/solution.py
@@ -2,6 +2,11 @@
 import jax.numpy as jnp
 from jax import lax
 from jax.sharding import PartitionSpec as P
+
+
+def add_all(x, mesh_axis):
+    parts = lax.all_gather(x, mesh_axis)
+    return jnp.sum(parts, axis=0)
 
 
 def local(features, v_weight, u_weight, cross_bias):
@@ -14,7 +19,7 @@
             lax.all_gather(v_weight[layer_number], "dp", axis=1, tiled=True),
             preferred_element_type=jnp.float32,
         )
-        rank_proj = lax.psum(partial_value, "mp").astype(jnp.bfloat16)
+        rank_proj = add_all(partial_value, "mp").astype(jnp.bfloat16)
         cross_term = jnp.dot(
             rank_proj,
             lax.all_gather(u_weight[layer_number], "dp", axis=0, tiled=True),

time: 554 us -> 815 us (1.47)
  waiting for transfers between devices: 49.3 us -> 712 us
  blocking collectives: 428 us -> 0 us
  other arithmetic: 0 us -> 25 us
    all_gather x0 -> x3, waiting for transfers between devices: none -> 461 us  [add_all(): parts = lax.all_gather(x, mesh_axis)]
    psum x3 -> x0, blocking collectives: 428 us -> none  [local(): rank_proj = lax.psum(partial_value, 'mp').astype(jnp.bfloat16)]
    all_gather x3, waiting for transfers between devices: 0.06 us -> 120 us  [local(): lax.all_gather(u_weight[layer_number], 'dp', axis=0, tiled=True)]
    all_gather x3, waiting for transfers between devices: 46.9 us -> 128 us  [local(): lax.all_gather(v_weight[layer_number], 'dp', axis=1, tiled=True)]
    reduce_sum x0 -> x3, other arithmetic: none -> 25 us  [add_all(): return jnp.sum(parts, axis=0)]
  transfers between devices with their start and end apart: 6 -> 9, of which waited for: 1 -> 9; matrix products, arithmetic and copies ran while one was open for 9% -> 6% of each run, Pallas kernels for 0% -> 0%
where the time goes in v1:
time: 815 us
  waiting for transfers between devices  712 us (87%)
  matrix products  58.9 us (7%)
  other arithmetic  25 us (3%)
  between operations  13.3 us (2%)
    all_gather x3, waiting for transfers between devices, add_all(): parts = lax.all_gather(x, mesh_axis)  461 us
    all_gather x3, waiting for transfers between devices, local(): lax.all_gather(v_weight[layer_number], 'dp', axis=1, tiled=True)  128 us
    all_gather x3, waiting for transfers between devices, local(): lax.all_gather(u_weight[layer_number], 'dp', axis=0, tiled=True)  120 us
    dot_general x3, matrix products, local(): jnp.dot(current, lax.all_gather(v_weight[layer_number], 'dp', axis=1, til...  29.8 us
    dot_general x3, matrix products, local(): jnp.dot(rank_proj, lax.all_gather(u_weight[layer_number], 'dp', axis=0, t...  29.1 us
    reduce_sum x3, other arithmetic, add_all(): return jnp.sum(parts, axis=0)  25 us
  transfers between devices with their start and end apart: 9, of which 9 were waited for; matrix products, arithmetic and copies ran while one was open for 6% of the time, Pallas kernels for 0%

profile of v1, /device:TPU:0, one launch (start us, length us, event | category | flops | bytes accessed | tf_op | source)
XLA Modules:
  0.0 814.8 jit_solution(11563156104398451564)
XLA Ops:
  6.5 0.0 all-gather.19.cloned.1.call-start
  6.5 2.6 fusion.26
  9.1 0.0 all-gather.19.cloned.1.call-update
  9.1 0.0 all-gather.21.cloned.1.call-start
  9.2 50.6 %all-gather.19.cloned.1.call-done = bf16[1,2048,1024]{2,1,0:T(8,128)(2,1)} async-done(((bf16[1,2048,128]{2,1,0:T(8,128)(2,1)}), bf16[1,2048,1024]{2,1,0:T(8,128)(2,1)}) %all-gather.19.cloned.1.call-update) | async-done | bytes 4194320 | tf_op jit(solution)/shard_map/all_gather | solution.py:19
  59.8 10.0 %fusion.15 = f32[1024,1024]{1,0:T(8,128)} fusion(bf16[1024,2048]{1,0:T(8,128)(2,1)} %param.4, bf16[1,2048,1024]{2,1,0:T(8,128)(2,1)} %all-gather.19.cloned.1.call-done), kind=kOutput, calls=%fused_computation.19 | convolution fusion | flops 4294967296 | bytes 12582912 | tf_op jit(solution)/shard_map/dot_general | solution.py:17
  69.8 0.0 copy-start
  69.8 0.0 copy-start.1
  69.8 0.0 all-gather.21.cloned.1.call-update
  69.8 0.0 all-gather.23.cloned.1.call-start
  69.9 1.3 copy-done
  71.2 1.2 fusion.27
  72.5 0.0 all-gather.23.cloned.1.call-update
  72.5 0.0 all-gather.25.cloned.1.call-start
  72.5 0.5 all-gather.25.cloned.1.call-update
  73.1 0.0 all-gather.27.cloned.1.call-start
  73.1 0.0 copy-done.1
  73.1 152.3 %all-gather.21.cloned.1.call-done = f32[4096,1024]{1,0:T(8,128)} async-done(((f32[1024,1024]{1,0:T(8,128)}), f32[4096,1024]{1,0:T(8,128)}) %all-gather.21.cloned.1.call-update) | async-done | bytes 16777232 | tf_op jit(solution)/shard_map/all_gather | solution.py:8
  225.5 8.3 %reduce_sum.27 = bf16[1024,1024]{1,0:T(8,128)(2,1)S(1)} reduce(f32[4,1024,1024]{2,1,0:T(8,128)} %bitcast.36, f32[]{:T(128)} %constant.0.clone.1), dimensions={0}, to_apply=%region_0.0 | reduce | flops 3145728 | bytes 18874372 | tf_op jit(solution)/shard_map/reduce_sum | solution.py:9
  233.8 40.2 %all-gather.23.cloned.1.call-done = bf16[1,1024,2048]{2,1,0:T(8,128)(2,1)} async-done(((bf16[1,128,2048]{2,1,0:T(8,128)(2,1)}), bf16[1,1024,2048]{2,1,0:T(8,128)(2,1)}) %all-gather.23.cloned.1.call-update) | async-done | bytes 4194320 | tf_op jit(solution)/shard_map/all_gather | solution.py:25
  274.0 9.3 %fusion = bf16[1024,2048]{1,0:T(8,128)(2,1)} fusion(bf16[1024,2048]{1,0:T(8,128)(2,1)} %param.4, f32[2048]{0:T(1024)S(1)} %bitcast.41, bf16[1,1024,2048]{2,1,0:T(8,128)(2,1)} %all-gather.23.cloned.1.call-done, bf16[1024,1024]{1,0:T(8,128)(2,1)S(1)} %reduce_sum.27), kind=kOutput, calls=%fused_computation.4 | convolution fusion | flops 4305453056 | bytes 14688256 | tf_op jit(solution)/shard_map/dot_general | solution.py:23
  283.3 38.8 %all-gather.25.cloned.1.call-done = bf16[1,2048,1024]{2,1,0:T(8,128)(2,1)} async-done(((bf16[1,2048,128]{2,1,0:T(8,128)(2,1)}), bf16[1,2048,1024]{2,1,0:T(8,128)(2,1)}) %all-gather.25.cloned.1.call-update) | async-done | bytes 4194320 | tf_op jit(solution)/shard_map/all_gather | solution.py:19
  322.1 9.9 %fusion.11 = f32[1024,1024]{1,0:T(8,128)} fusion(bf16[1024,2048]{1,0:T(8,128)(2,1)} %fusion, bf16[1,2048,1024]{2,1,0:T(8,128)(2,1)} %all-gather.25.cloned.1.call-done), kind=kOutput, calls=%fused_computation.15 | convolution fusion | flops 4294967296 | bytes 12582912 | tf_op jit(solution)/shard_map/dot_general | solution.py:17
  332.0 0.0 all-gather.27.cloned.1.call-update
  332.0 0.0 all-gather.29.cloned.1.call-start
  332.1 0.5 all-gather.29.cloned.1.call-update
  332.6 0.0 all-gather.31.cloned.1.call-start
  332.7 0.7 all-gather.31.cloned.1.call-update
  333.4 0.2 all-gather.33.cloned.1.call-start
  333.6 154.1 %all-gather.27.cloned.1.call-done = f32[4096,1024]{1,0:T(8,128)} async-done(((f32[1024,1024]{1,0:T(8,128)}), f32[4096,1024]{1,0:T(8,128)}) %all-gather.27.cloned.1.call-update) | async-done | bytes 16777232 | tf_op jit(solution)/shard_map/all_gather | solution.py:8
  487.7 8.3 %reduce_sum.28 = bf16[1024,1024]{1,0:T(8,128)(2,1)S(1)} reduce(f32[4,1024,1024]{2,1,0:T(8,128)} %bitcast.37, f32[]{:T(128)} %constant.0.clone.1), dimensions={0}, to_apply=%region_1.0 | reduce | flops 3145728 | bytes 18874372 | tf_op jit(solution)/shard_map/reduce_sum | solution.py:9
  496.0 40.0 %all-gather.29.cloned.1.call-done = bf16[1,1024,2048]{2,1,0:T(8,128)(2,1)} async-done(((bf16[1,128,2048]{2,1,0:T(8,128)(2,1)}), bf16[1,1024,2048]{2,1,0:T(8,128)(2,1)}) %all-gather.29.cloned.1.call-update) | async-done | bytes 4194320 | tf_op jit(solution)/shard_map/all_gather | solution.py:25
  536.0 9.9 %fusion.2 = bf16[1024,2048]{1,0:T(8,128)(2,1)} fusion(bf16[1024,2048]{1,0:T(8,128)(2,1)} %param.4, bf16[1024,2048]{1,0:T(8,128)(2,1)} %fusion, f32[2048]{0:T(1024)S(1)} %bitcast.40, bf16[1,1024,2048]{2,1,0:T(8,128)(2,1)} %all-gather.29.cloned.1.call-done, bf16[1024,1024]{1,0:T(8,128)(2,1)S(1)} %reduce_sum.28), kind=kOutput, calls=%fused_computation.6 | convolution fusion | flops 4307550208 | bytes 18882560 | tf_op jit(solution)/shard_map/dot_general | solution.py:23
  545.9 38.4 %all-gather.31.cloned.1.call-done = bf16[1,2048,1024]{2,1,0:T(8,128)(2,1)} async-done(((bf16[1,2048,128]{2,1,0:T(8,128)(2,1)}), bf16[1,2048,1024]{2,1,0:T(8,128)(2,1)}) %all-gather.31.cloned.1.call-update) | async-done | bytes 4194320 | tf_op jit(solution)/shard_map/all_gather | solution.py:19
  584.3 10.0 %fusion.7 = f32[1024,1024]{1,0:T(8,128)} fusion(bf16[1024,2048]{1,0:T(8,128)(2,1)} %fusion.2, bf16[1,2048,1024]{2,1,0:T(8,128)(2,1)} %all-gather.31.cloned.1.call-done), kind=kOutput, calls=%fused_computation.11 | convolution fusion | flops 4294967296 | bytes 12582912 | tf_op jit(solution)/shard_map/dot_general | solution.py:17
  594.2 0.0 all-gather.33.cloned.1.call-update
  594.2 0.3 all-gather.35.cloned.1.call-start
  594.5 0.5 all-gather.35.cloned.1.call-update
  595.0 154.9 %all-gather.33.cloned.1.call-done = f32[4096,1024]{1,0:T(8,128)} async-done(((f32[1024,1024]{1,0:T(8,128)}), f32[4096,1024]{1,0:T(8,128)}) %all-gather.33.cloned.1.call-update) | async-done | bytes 16777232 | tf_op jit(solution)/shard_map/all_gather | solution.py:8
  749.9 8.3 %reduce_sum.29 = bf16[1024,1024]{1,0:T(8,128)(2,1)S(1)} reduce(f32[4,1024,1024]{2,1,0:T(8,128)} %bitcast.38, f32[]{:T(128)} %constant.0.clone.1), dimensions={0}, to_apply=%region_2.0 | reduce | flops 3145728 | bytes 18874372 | tf_op jit(solution)/shard_map/reduce_sum | solution.py:9
  758.2 40.2 %all-gather.35.cloned.1.call-done = bf16[1,1024,2048]{2,1,0:T(8,128)(2,1)} async-done(((bf16[1,128,2048]{2,1,0:T(8,128)(2,1)}), bf16[1,1024,2048]{2,1,0:T(8,128)(2,1)}) %all-gather.35.cloned.1.call-update) | async-done | bytes 4194320 | tf_op jit(solution)/shard_map/all_gather | solution.py:25
  798.4 9.9 %fusion.4 = bf16[1024,2048]{1,0:T(8,128)(2,1)} fusion(bf16[1024,2048]{1,0:T(8,128)(2,1)} %param.4, bf16[1024,2048]{1,0:T(8,128)(2,1)} %fusion.2, f32[2048]{0:T(1024)S(1)} %bitcast.39, bf16[1,1024,2048]{2,1,0:T(8,128)(2,1)} %all-gather.35.cloned.1.call-done, bf16[1024,1024]{1,0:T(8,128)(2,1)S(1)} %reduce_sum.29), kind=kOutput, calls=%fused_computation.8 | convolution fusion | flops 4307550208 | bytes 18882560 | tf_op jit(solution)/shard_map/dot_general | solution.py:23
  (1 shorter events, 0.0 us)
Async XLA Ops:
  6.5 53.3 %all-gather.19.cloned.1.call-start = ((), (), s32[]{:S(2)}) async-start(), calls=%async_computation | async-start | bytes 4718592 | tf_op jit(solution)/shard_map/all_gather | solution.py:19
  9.1 216.3 %all-gather.21.cloned.1.call-start = ((), (), s32[]{:S(2)}) async-start(), calls=%async_computation.1 | async-start | bytes 20971520 | tf_op jit(solution)/shard_map/all_gather | solution.py:8
  69.8 1.4 copy-start
  69.8 3.3 copy-start.1
  69.8 204.1 %all-gather.23.cloned.1.call-start = ((), (), s32[]{:S(2)}) async-start(), calls=%async_computation.2 | async-start | bytes 4718592 | tf_op jit(solution)/shard_map/all_gather | solution.py:25
  72.5 249.6 %all-gather.25.cloned.1.call-start = ((), (), s32[]{:S(2)}) async-start(), calls=%async_computation.3 | async-start | bytes 4718592 | tf_op jit(solution)/shard_map/all_gather | solution.py:19
  73.1 414.6 %all-gather.27.cloned.1.call-start = ((), (), s32[]{:S(2)}) async-start(), calls=%async_computation.4 | async-start | bytes 20971520 | tf_op jit(solution)/shard_map/all_gather | solution.py:8
  332.0 204.0 %all-gather.29.cloned.1.call-start = ((), (), s32[]{:S(2)}) async-start(), calls=%async_computation.5 | async-start | bytes 4718592 | tf_op jit(solution)/shard_map/all_gather | solution.py:25
  332.6 251.6 %all-gather.31.cloned.1.call-start = ((), (), s32[]{:S(2)}) async-start(), calls=%async_computation.6 | async-start | bytes 4718592 | tf_op jit(solution)/shard_map/all_gather | solution.py:19
  333.4 416.5 %all-gather.33.cloned.1.call-start = ((), (), s32[]{:S(2)}) async-start(), calls=%async_computation.7 | async-start | bytes 20971520 | tf_op jit(solution)/shard_map/all_gather | solution.py:8
  594.2 204.1 %all-gather.35.cloned.1.call-start = ((), (), s32[]{:S(2)}) async-start(), calls=%async_computation.8 | async-start | bytes 4718592 | tf_op jit(solution)/shard_map/all_gather | solution.py:25
Sparse Core Ops, SparseCore 0:
  9.3 50.5 all-gather.18
  70.0 155.4 all-gather.20
  227.1 46.8 all-gather.22
  275.4 46.6 all-gather.24
  332.2 155.4 all-gather.26
  489.1 46.8 all-gather.28
  537.6 46.6 all-gather.30
  594.4 155.4 all-gather.32
  751.5 46.8 all-gather.34
